TPU v7x, 32 devices: a whole 2x2x4 slice. The times are simulated.
32 devices in a mesh: grp: 4 (over z), loc: 8 (over y, x, core).
Axes of the slice: x: 2, y: 2, z: 4, core: 2. Of those that a mesh axis runs over, the one named last changes fastest.
Arguments:
- features: float32 [32768, 256], P(('grp', 'loc')), may hold values from -6 to 6
- hub_block: bfloat16 [128, 32768], P(None, ('grp', 'loc')), may hold values from -0.0625 to 0.0625
- hub_slot: int32 [128], P(('grp', 'loc')), may hold values from 0 to 1023, as said below
- neighbours: int32 [32768, 16], P(('grp', 'loc')), may hold values from 0 to 2047
- counts: int32 [32768], P(('grp', 'loc')), may hold values from 1 to 16
- halo_send: int32 [256, 128], P(('grp', 'loc')), may hold values from 0 to 1023
- weight: float32 [256, 256], replicated, may hold values from -0.375 to 0.375
- bias: float32 [256], replicated, may hold values from -3 to 3
Outputs:
- layer_out: float32 [32768, 256], P(('grp', 'loc'))
Inputs may be any that keep to these rules, and one draw needn't show every extreme that they name: `hub_slot`: within each aligned block of 4 entries the values are distinct.
All inputs are finite; a program needn't handle non-finite values.
Results may differ from a plain program's by a relative error of at most 0.0003.
Values sent between devices are 32-bit elements; how exact they have to be, the bound alone decides.
A program may use at most 64 MiB of HBM per device.

v0:
```python
import jax
import jax.numpy as jnp
from jax import lax
from jax.sharding import PartitionSpec as P


def on_device(features, hub_block, hub_slot, neighbours, counts, halo_send, weight, bias):
    width = features.shape[1]
    own_rows = features.shape[0]
    slot_total = neighbours.shape[1]
    rounded = features.astype(jnp.bfloat16)
    group_part = lax.psum_scatter(
        jnp.dot(hub_block, rounded, preferred_element_type=jnp.float32),
        "grp",
        scatter_dimension=0,
        tiled=True,
    )
    hub_part = lax.psum_scatter(group_part, "loc", scatter_dimension=0, tiled=True)
    outgoing = features[halo_send.reshape(-1)]
    outgoing = outgoing.reshape(halo_send.shape[0], halo_send.shape[1], width)
    received = lax.all_to_all(outgoing, "loc", split_axis=0, concat_axis=0, tiled=True)
    pooled = jnp.concatenate([features, received.reshape(-1, width)], axis=0)
    pool_rows = pooled.shape[0]
    block_rows = 512
    block_count = own_rows // block_rows
    pool_index = jnp.arange(pool_rows, dtype=jnp.int32)

    def block_sum(pair):
        slots, used_counts = pair
        adjacency = jnp.zeros((slots.shape[0], pool_rows), jnp.float32)
        for slot_number in range(slot_total):
            active = (slot_number < used_counts)[:, None]
            hits = (slots[:, slot_number][:, None] == pool_index[None, :]) & active
            adjacency = adjacency + hits.astype(jnp.float32)
        summed = jnp.dot(
            adjacency, pooled, precision=lax.Precision.HIGHEST, preferred_element_type=jnp.float32
        )
        return summed / used_counts.astype(jnp.float32)[:, None]

    low = lax.map(
        block_sum,
        (
            neighbours.reshape(block_count, block_rows, slot_total),
            counts.reshape(block_count, block_rows),
        ),
    )
    low = low.reshape(own_rows, width)
    own_index = jnp.arange(own_rows, dtype=jnp.int32)
    hub_place = (own_index[:, None] == hub_slot[None, :]).astype(jnp.float32)
    hub_rows = jnp.dot(
        hub_place, hub_part, precision=lax.Precision.HIGHEST, preferred_element_type=jnp.float32
    )
    combined = features + low + hub_rows
    result = (
        jnp.dot(
            combined, weight, precision=lax.Precision.HIGHEST, preferred_element_type=jnp.float32
        )
        + bias
    )
    return jnp.maximum(result, 0.0)


def solution(mesh):
    in_specs = (
        P(("grp", "loc"), None),
        P(None, ("grp", "loc")),
        P(("grp", "loc")),
        P(("grp", "loc"), None),
        P(("grp", "loc")),
        P(("grp", "loc"), None),
        P(),
        P(),
    )
    out_specs = P(("grp", "loc"), None)
    return jax.shard_map(
        on_device, mesh=mesh, in_specs=in_specs, out_specs=out_specs, check_vma=False
    )
```

profile of v0, /device:TPU:0, one launch (start us, length us, event | category | flops | bytes accessed | tf_op | source)
XLA Modules:
  0.0 113.5 jit_solution(5485420684897665984)
XLA Ops:
  6.5 0.0 copy-start
  6.5 0.7 compare_select_fusion
  7.3 5.9 %gather_fusion = f32[1024,256]{1,0:T(8,128)} fusion(f32[1024,256]{1,0:T(8,128)} %param.10, s32[1024]{0:T(1024)S(1)} %broadcast_clamp_fusion), kind=kCustom, calls=%fused_computation | custom fusion | bytes 2101248 | tf_op jit(solution)/shard_map/gather | solution.py:19
  13.2 0.0 copy-start.1
  13.2 0.0 copy-start.2
  13.2 0.0 copy-start.3
  13.2 0.0 copy-start.4
  13.2 0.0 copy-start.7
  13.2 5.3 %all-to-all-start = ((f32[8,128,256]{2,1,0:T(8,128)}), f32[8,128,256]{2,1,0:T(8,128)S(1)}, u32[]{:S(2)}, u32[]{:S(2)}) async-start(f32[8,128,256]{2,1,0:T(8,128)} %bitcast.2), calls=%async_computation | async-start | bytes 2097152 | tf_op jit(solution)/shard_map/all_to_all | solution.py:21
  18.6 0.0 reduce-scatter.2.cloned.1.call-start
  18.6 0.0 copy-done.1
  18.6 0.0 copy-done.2
  18.6 0.9 fusion.108
  19.5 0.0 reduce-scatter.2.cloned.1.call-update
  19.5 0.0 copy-done.3
  19.5 0.1 reshape.167
  19.6 0.0 copy-done.4
  19.6 0.0 copy-done.7
  19.6 0.6 dynamic-slice
  20.9 21.9 %reduce-scatter.2.cloned.1.call-done = f32[32,256]{1,0:T(8,128)} async-done(((f32[128,256]{1,0:T(8,128)}), f32[32,256]{1,0:T(8,128)}) %reduce-scatter.2.cloned.1.call-update) | async-done | bytes 32784 | tf_op jit(solution)/shard_map/reduce_scatter | solution.py:12
  42.8 22.9 %all-reduce = f32[32,256]{1,0:T(8,128)S(1)} all-reduce(f32[32,256]{1,0:T(8,128)} %reduce-scatter.2.cloned.1.call-done), channel_id=3, replica_groups=mesh['grp'=4,'loc'=8] {'loc'}, use_global_device_ids=true, to_apply=%region_3.4.clone | all-reduce | flops 8192 | bytes 65536
  65.7 0.0 all-to-all-done
  65.7 1.5 %pad_maximum_fusion = f32[2048,256]{1,0:T(8,128)} fusion(f32[1024,256]{1,0:T(8,128)S(1)} %bitcast.77, f32[1024,256]{1,0:T(8,128)S(1)} %copy-done.1), kind=kLoop, calls=%fused_computation.120 | loop fusion | flops 524288 | bytes 4194304 | tf_op jit(solution)/shard_map/concatenate | solution.py:22
  67.2 36.3 %while.12 = (s32[]{:T(128)}, f32[2,512,256]{2,1,0:T(8,128)S(1)}, s32[2,512,16]{1,0,2:T(2,128)S(1)}, s32[2,512]{1,0:T(2,128)S(1)}, f32[2048,256]{1,0:T(8,128)}, /*index=5*/s32[]{:T(128)}) while((s32[]{:T(128)}, f32[2,512,256]{2,1,0:T(8,128)S(1)}, s32[2,512,16]{1,0,2:T(2,128)S(1)}, s32[2,512]{1,0:T(2,128)S(1)}, ...), condition=%wide.region_1.0_spmd.clone.clone, body=%wide.region_0.0_spmd.clone.clone.sunk | while | flops 3287425536 | bytes 2877521 | solution.py:40
  67.2 0.1 compare_reduce_fusion.17
  67.4 17.9 %fusion.128 = f32[2,512,256]{2,1,0:T(8,128)S(1)} fusion(f32[2,512,256]{2,1,0:T(8,128)S(1)} %get-tuple-element.285, s32[]{:T(128)} %get-tuple-element.284, f32[2048,256]{1,0:T(8,128)} %get-tuple-element.294, s32[512]{0:T(512)S(1)} %bitcast.80, s32[512]{0:T(512)S(1)} %bitcast.81, s32[512]{0:T(512)S(1)} %bitcast.82, s32[512]{0:T(512)S(1)} %bitcast.83, ...), kind=kOutput, calls=%fused_computation.100.clone.1 | convolution fusion | flops 3287416832 | bytes 2664452 | tf_op jit(solution)/shard_map/while/body/eval_jaxpr/dot_general | solution.py:35
  85.3 0.1 compare_reduce_fusion.17
  85.5 17.9 %fusion.128 = f32[2,512,256]{2,1,0:T(8,128)S(1)} fusion(f32[2,512,256]{2,1,0:T(8,128)S(1)} %get-tuple-element.285, s32[]{:T(128)} %get-tuple-element.284, f32[2048,256]{1,0:T(8,128)} %get-tuple-element.294, s32[512]{0:T(512)S(1)} %bitcast.80, s32[512]{0:T(512)S(1)} %bitcast.81, s32[512]{0:T(512)S(1)} %bitcast.82, s32[512]{0:T(512)S(1)} %bitcast.83, ...), kind=kOutput, calls=%fused_computation.100.clone.1 | convolution fusion | flops 3287416832 | bytes 2664452 | tf_op jit(solution)/shard_map/while/body/eval_jaxpr/dot_general | solution.py:35
  103.5 0.0 copy-start.6
  103.5 0.0 copy-start.5
  103.5 0.1 bitcast_add_fusion
  103.6 0.5 copy-done.6
  104.1 0.6 convolution_add_fusion
  104.7 0.0 copy-done
  104.7 0.0 copy-done.5
  104.7 2.0 %fusion.107 = f32[1024,256]{1,0:T(8,128)} fusion(f32[1024,256]{1,0:T(8,128)S(1)} %convolution_add_fusion, f32[256,256]{1,0:T(8,128)S(1)} %copy-done, f32[256]{0:T(256)S(1)} %copy-done.5), kind=kOutput, calls=%fused_computation.123 | convolution fusion | flops 805830656 | bytes 2360320 | tf_op jit(solution)/shard_map/dot_general | solution.py:55
  (11 shorter events, 0.2 us)
Async XLA Ops:
  6.5 98.2 %copy-start = (f32[256,256]{1,0:T(8,128)S(1)}, f32[256,256]{1,0:T(8,128)}, u32[]{:S(2)}) copy-start(f32[256,256]{1,0:T(8,128)} %param.16) | copy-start | bytes 786436
  13.2 5.4 %copy-start.1 = (f32[1024,256]{1,0:T(8,128)S(1)}, f32[1024,256]{1,0:T(8,128)}, u32[]{:S(2)}) copy-start(f32[1024,256]{1,0:T(8,128)} %param.10) | copy-start | bytes 3145732
  13.2 5.4 %copy-start.2 = (bf16[128,1024]{1,0:T(8,128)(2,1)S(1)}, bf16[128,1024]{1,0:T(8,128)(2,1)}, u32[]{:S(2)}) copy-start(bf16[128,1024]{1,0:T(8,128)(2,1)} %param.11) | copy-start | bytes 786436
  13.2 6.3 %copy-start.3 = (s32[1024,16]{0,1:T(8,128)S(1)}, s32[1024,16]{0,1:T(8,128)}, u32[]{:S(2)}) copy-start(s32[1024,16]{0,1:T(8,128)} %param.13) | copy-start | bytes 196612
  13.2 6.4 %copy-start.4 = (s32[1024]{0:T(1024)S(1)}, s32[1024]{0:T(1024)}, u32[]{:S(2)}) copy-start(s32[1024]{0:T(1024)} %param.14) | copy-start | bytes 12292
  13.2 6.4 %copy-start.7 = (u32[32]{0:T(128)S(1)}, u32[32]{0:T(128)}, u32[]{:S(2)}) copy-start(u32[32]{0:T(128)} %constant.53) | copy-start | bytes 388
  13.2 52.5 %all-to-all-start = ((f32[8,128,256]{2,1,0:T(8,128)}), f32[8,128,256]{2,1,0:T(8,128)S(1)}, u32[]{:S(2)}, u32[]{:S(2)}) async-start(f32[8,128,256]{2,1,0:T(8,128)} %bitcast.2), calls=%async_computation | async-start | bytes 2097152 | tf_op jit(solution)/shard_map/all_to_all | solution.py:21
  18.6 24.2 %reduce-scatter.2.cloned.1.call-start = ((), (), s32[]{:S(2)}) async-start(), calls=%async_computation.2 | async-start | bytes 163840 | tf_op jit(solution)/shard_map/reduce_scatter | solution.py:12
  103.5 0.7 copy-start.6
  103.5 1.2 %copy-start.5 = (f32[256]{0:T(256)S(1)}, f32[256]{0:T(256)}, u32[]{:S(2)}) copy-start(f32[256]{0:T(256)} %param.17) | copy-start | bytes 3076
Sparse Core Ops, SparseCore 0:
  21.6 21.1 reduce-scatter.1
where the time goes:
time: 114 us
  matrix products  39.2 us (34%)
  blocking collectives  22.9 us (20%)
  waiting for transfers between devices  21.9 us (19%)
  between operations  14.2 us (12%)
  local copies, waits for them, and re-layouts  7.26 us (6%)
  starting transfers between devices  5.38 us (5%)
  other arithmetic  2.58 us (2%)
    dot_general x2, matrix products, block_sum(): jnp.dot(adjacency, pooled, precision=lax.Precision.HIGHEST, preferred_ele...  35.8 us
    unnamed x1, blocking collectives  22.9 us
    reduce_scatter x1, waiting for transfers between devices, on_device(): lax.psum_scatter(jnp.dot(hub_block, rounded, preferred_element_type=jnp.f...  21.9 us
    gather x1, local copies, waits for them, and re-layouts, on_device(): outgoing = features[halo_send.reshape(-1)]  5.9 us
    all_to_all x1, starting transfers between devices, on_device(): lax.all_to_all(outgoing, 'loc', split_axis=0, concat_axis=0, tiled=True)  5.34 us
  transfers between devices with their start and end apart: 2, of which 1 were waited for; matrix products, arithmetic and copies ran while one was open for 1% of the time, Pallas kernels for 0%

commit v1 on v0

v1 whole, which is shorter than its diff:
```python
import functools

import jax
import jax.numpy as jnp
from jax import lax
from jax.experimental import pallas as pl
from jax.experimental.pallas import tpu as pltpu
from jax.sharding import PartitionSpec as P

BF = jnp.bfloat16
F32 = jnp.float32
LANES = 128


def flip(index, mask, count):
    result = index
    bit = 1
    while bit < count:
        if mask & bit:
            result = result + bit * (1 - 2 * ((index // bit) % 2))
        bit *= 2
    return result


def send_order(count):
    far = [off for off in range(2, count) if bin(off >> 1).count("1") > 1]
    near = [off for off in range(2, count) if bin(off >> 1).count("1") == 1][::-1]
    order = []
    while far or near:
        if far:
            order.append(far.pop(0))
        if near:
            order.append(near.pop(0))
    return order + [1]


def dot(a, b):
    return jnp.dot(a, b, preferred_element_type=F32)


def dot_nt(a, b):
    return lax.dot_general(a, b, (((1,), (1,)), ((), ())), preferred_element_type=F32)


def split(x):
    high = x.astype(BF)
    return high, (x - high.astype(F32)).astype(BF)


def onehot(mask):
    return jnp.where(mask, 1.0, 0.0).astype(BF)


def iota(shape, dim):
    return lax.broadcasted_iota(jnp.int32, shape, dim)


def kernel(
    n_grp, n_loc,
    feat_ref, hub_ref, slot_ref, nbr_ref, cnt_ref, halo_ref, w_ref, bias_ref,
    out_ref,
    fh, fl, ph, pl_, base, acc, adj, codes, lows, outgoing, recv, part, part_in, spread, spread_in,
    inv, wh, wl,
    halo_s, halo_r, grp_s, grp_r, loc_s, loc_r,
):
    grp = lax.axis_index("grp")
    me = lax.axis_index("loc")
    rows, width = feat_ref.shape
    listed = halo_ref.shape[1]
    slots = nbr_ref.shape[0]
    hub_grp = hub_ref.shape[0] // n_grp
    hub_dev = slot_ref.shape[0]
    levels = rows // LANES + n_loc * listed // LANES
    per_block = 256 // slots
    blocks = rows // per_block

    barrier = pltpu.get_barrier_semaphore()
    for off in range(1, n_loc):
        pl.semaphore_signal(
            barrier, inc=1, device_id={"loc": flip(me, off, n_loc)}, device_id_type=pl.DeviceIdType.MESH
        )
    for off in range(1, n_grp):
        pl.semaphore_signal(
            barrier, inc=1, device_id={"grp": (grp + off) % n_grp}, device_id_type=pl.DeviceIdType.MESH
        )

    high, low = split(feat_ref[...])
    fh[...] = high
    fl[...] = low
    part[...] = dot(hub_ref[...], fh[...])

    def gather(peer):
        line = halo_ref[pl.ds(peer, 1), :]
        column = jnp.transpose(jnp.broadcast_to(line, (LANES, listed)).astype(F32)).astype(jnp.int32)
        lane = iota((listed, LANES), 1)
        pick = jnp.concatenate(
            [onehot(column == lane + tile * LANES) for tile in range(rows // LANES)], axis=1
        )
        return dot(pick, fh[...]) + dot(pick, fl[...])

    def halo_copy(off):
        return pltpu.make_async_remote_copy(
            src_ref=outgoing.at[off],
            dst_ref=recv.at[pl.ds(pl.multiple_of(me * listed, listed), listed)],
            send_sem=halo_s.at[off],
            recv_sem=halo_r.at[off],
            device_id={"loc": flip(me, off, n_loc)},
            device_id_type=pl.DeviceIdType.MESH,
        )

    def grp_copy(off):
        target = (grp + off) % n_grp
        return pltpu.make_async_remote_copy(
            src_ref=part.at[pl.ds(pl.multiple_of(target * hub_grp, hub_grp), hub_grp)],
            dst_ref=part_in.at[off],
            send_sem=grp_s.at[off],
            recv_sem=grp_r.at[off],
            device_id={"grp": target},
            device_id_type=pl.DeviceIdType.MESH,
        )

    def loc_copy(off):
        target = flip(me, off, n_loc)
        return pltpu.make_async_remote_copy(
            src_ref=spread.at[target],
            dst_ref=spread_in.at[off],
            send_sem=loc_s.at[off],
            recv_sem=loc_r.at[off],
            device_id={"loc": target},
            device_id_type=pl.DeviceIdType.MESH,
        )

    order = send_order(n_loc)
    outgoing[order[0]] = gather(flip(me, order[0], n_loc))
    pl.semaphore_wait(barrier, n_loc - 1 + n_grp - 1)
    halo_copy(order[0]).start()
    for off in range(1, n_grp):
        grp_copy(off).start()
    for off in order[1:]:
        outgoing[off] = gather(flip(me, off, n_loc))
        halo_copy(off).start()
    recv[pl.ds(pl.multiple_of(me * listed, listed), listed), :] = gather(me)

    slot = nbr_ref[...]
    used = iota((slots, rows), 0) < jnp.broadcast_to(cnt_ref[...], (slots, rows))
    level = jnp.where(used, lax.shift_right_logical(slot, 7), -16).astype(F32)
    place = jnp.where(used, slot & (LANES - 1), 0).astype(F32)
    spots = (iota((rows, 256), 0) % per_block) == (iota((rows, 256), 1) % per_block)
    repeat = onehot(iota((slots, 256), 1) // per_block == iota((slots, 256), 0))
    member = onehot(iota((blocks, rows), 1) // per_block == iota((blocks, rows), 0))

    def flatten(table):
        spread_out = dot(jnp.transpose(table).astype(BF), repeat)
        return dot(member, jnp.where(spots, spread_out, 0.0).astype(BF))

    codes[...] = flatten(level).astype(jnp.int32) * per_block + iota((blocks, 256), 1) % per_block
    lows[...] = flatten(place).astype(jnp.int32)
    inv[...] = 1.0 / jnp.transpose(jnp.broadcast_to(cnt_ref[...].astype(F32), (8, rows)))

    w_high, w_low = split(w_ref[...])
    wh[...] = w_high
    wl[...] = w_low

    def times_weight(x_high, x_low):
        return dot(x_high, wh[...]) + dot(x_low, wh[...]) + dot(x_high, wl[...])

    product = times_weight(fh[...], fl[...])
    base[...] = product + bias_ref[...]
    p_high, p_low = split(product)
    ph[...] = p_high
    pl_[...] = p_low

    group = 4

    def build(step, carry):
        for inner in range(group):
            block = step * group + inner
            code = codes[pl.ds(block, 1), :]
            spot = lows[pl.ds(block, 1), :]
            left = onehot(iota((levels * per_block, 256), 0) == code)
            right = onehot(iota((LANES, 256), 0) == spot)
            counted = dot_nt(left, right).astype(BF)
            at = pl.ds(pl.multiple_of(block * per_block, per_block), per_block)
            for tile in range(levels):
                adj[tile // 2, at, (tile % 2) * LANES:(tile % 2 + 1) * LANES] = counted[
                    tile * per_block:(tile + 1) * per_block
                ]
        return carry

    lax.fori_loop(0, blocks // group, build, 0)

    own = rows // 256
    total = dot(adj[0], ph[0:256]) + dot(adj[0], pl_[0:256])
    for chunk in range(1, own):
        at = slice(chunk * 256, (chunk + 1) * 256)
        total = total + dot(adj[chunk], ph[at]) + dot(adj[chunk], pl_[at])
    acc[...] = total

    for off in range(1, n_grp):
        grp_copy(off).wait_recv()
    group_sum = part[pl.ds(pl.multiple_of(grp * hub_grp, hub_grp), hub_grp), :]
    for off in range(1, n_grp):
        group_sum = group_sum + part_in[off]
    spread[...] = jnp.zeros_like(spread)
    for owner in range(n_loc):
        spread[owner, 0:hub_dev, :] = group_sum[owner * hub_dev:(owner + 1) * hub_dev]
    for off in range(1, n_loc):
        loc_copy(off).start()

    def take(chip_off):
        chip = flip(me // 2, chip_off, n_loc // 2)
        got = recv[pl.ds(pl.multiple_of(chip * 2 * listed, 2 * listed), 2 * listed), :]
        r_high, r_low = split(times_weight(*split(got)))
        counts_of = adj[own + chip]
        return dot(counts_of, r_high) + dot(counts_of, r_low)

    chips = [0]
    for off in order:
        if off // 2 not in chips:
            chips.append(off // 2)
    halo_copy(1).wait_recv()
    for chip_off in chips[:-1]:
        if chip_off > 0:
            halo_copy(2 * chip_off).wait_recv()
            halo_copy(2 * chip_off + 1).wait_recv()
        acc[...] += take(chip_off)

    hubs = spread[me]
    for off in range(1, n_loc):
        loc_copy(off).wait_recv()
        hubs = hubs + spread_in[off]
    hubs = jnp.concatenate([hubs, jnp.zeros((LANES - hubs.shape[0], width), F32)], axis=0)
    h_high, h_low = split(times_weight(*split(hubs)))
    lane = iota((1, LANES), 1)
    target_row = jnp.full((1, LANES), -1, jnp.int32)
    for hub in range(hub_dev):
        target_row = jnp.where(lane == hub, slot_ref[hub], target_row)
    here = onehot(iota((rows, LANES), 0) == target_row)
    base[...] += dot(here, h_high) + dot(here, h_low)

    last = chips[-1]
    halo_copy(2 * last).wait_recv()
    halo_copy(2 * last + 1).wait_recv()
    out_ref[...] = jnp.maximum((acc[...] + take(last)) * inv[:, 0:1] + base[...], 0.0)

    for off in range(1, n_loc):
        halo_copy(off).wait_send()
        loc_copy(off).wait_send()
    for off in range(1, n_grp):
        grp_copy(off).wait_send()


def solution(mesh):
    n_grp, n_loc = mesh.shape["grp"], mesh.shape["loc"]

    def on_device(features, hub_block, hub_slot, neighbours, counts, halo_send, weight, bias):
        rows, width = features.shape
        slots = neighbours.shape[1]
        listed = halo_send.shape[1]
        hubs = hub_block.shape[0]
        pool = rows + n_loc * listed
        blocks = rows // (256 // slots)
        padded = -(-hub_slot.shape[0] // 8) * 8
        vmem = pl.BlockSpec(memory_space=pltpu.VMEM)
        smem = pl.BlockSpec(memory_space=pltpu.SMEM)
        sem = pltpu.SemaphoreType.DMA
        return pl.pallas_call(
            functools.partial(kernel, n_grp, n_loc),
            out_shape=jax.ShapeDtypeStruct((rows, width), F32),
            in_specs=[vmem, vmem, smem, vmem, vmem, vmem, vmem, vmem],
            out_specs=vmem,
            scratch_shapes=[
                pltpu.VMEM((rows, width), BF),
                pltpu.VMEM((rows, width), BF),
                pltpu.VMEM((rows, width), BF),
                pltpu.VMEM((rows, width), BF),
                pltpu.VMEM((rows, width), F32),
                pltpu.VMEM((rows, width), F32),
                pltpu.VMEM((pool // 256, rows, 256), BF),
                pltpu.VMEM((blocks, 256), jnp.int32),
                pltpu.VMEM((blocks, 256), jnp.int32),
                pltpu.VMEM((n_loc, listed, width), F32),
                pltpu.VMEM((n_loc * listed, width), F32),
                pltpu.VMEM((hubs, width), F32),
                pltpu.VMEM((n_grp, hubs // n_grp, width), F32),
                pltpu.VMEM((n_loc, padded, width), F32),
                pltpu.VMEM((n_loc, padded, width), F32),
                pltpu.VMEM((rows, 8), F32),
                pltpu.VMEM(weight.shape, BF),
                pltpu.VMEM(weight.shape, BF),
                sem((n_loc,)), sem((n_loc,)), sem((n_grp,)), sem((n_grp,)), sem((n_loc,)), sem((n_loc,)),
            ],
            compiler_params=pltpu.CompilerParams(
                collective_id=0, has_side_effects=True, vmem_limit_bytes=48 * 1024 * 1024
            ),
        )(
            features, hub_block, hub_slot, neighbours.T, counts.reshape(1, -1), halo_send, weight,
            bias.reshape(1, -1),
        )

    both = ("grp", "loc")
    return jax.shard_map(
        on_device,
        mesh=mesh,
        in_specs=(P(both, None), P(None, both), P(both), P(both, None), P(both), P(both, None), P(), P()),
        out_specs=P(both, None),
        check_vma=False,
    )
```

time: 114 us -> 30.6 us (0.27)
  matrix products: 39.2 us -> 0 us
  Pallas kernels: 0 us -> 23.9 us
  blocking collectives: 22.9 us -> 0 us
  waiting for transfers between devices: 21.9 us -> 0 us
  between operations: 14.2 us -> 0.02 us
  starting transfers between devices: 5.38 us -> 0 us
  other arithmetic: 2.58 us -> 0 us
    dot_general x5 -> x0, matrix products: 39.2 us -> none  [the longest x2 35.8 us: block_sum(): jnp.dot(adjacency, pooled, precision=lax.Precision.HIGHEST, preferred_ele...]
    pallas_call x0 -> x1, Pallas kernels: none -> 23.9 us  [on_device(): pl.pallas_call(functools.partial(kernel, n_grp, n_loc), out_shape=jax.Sha...]
    unnamed x1 -> x0, blocking collectives: 22.9 us -> none
    reduce_scatter x1 -> x0, waiting for transfers between devices: 21.9 us -> none  [on_device(): lax.psum_scatter(jnp.dot(hub_block, rounded, preferred_element_type=jnp.f...]
    gather x1 -> x0, local copies, waits for them, and re-layouts: 5.9 us -> none  [on_device(): outgoing = features[halo_send.reshape(-1)]]
    all_to_all x1 -> x0, starting transfers between devices: 5.34 us -> none  [on_device(): lax.all_to_all(outgoing, 'loc', split_axis=0, concat_axis=0, tiled=True)]
    unnamed x17, local copies, waits for them, and re-layouts: 1.16 us -> 6.32 us
    concatenate x1 -> x0, other arithmetic: 1.49 us -> none  [on_device(): pooled = jnp.concatenate([features, received.reshape(-1, width)], axis=0)]
  transfers between devices with their start and end apart: 2 -> 0, of which waited for: 1 -> 0; matrix products, arithmetic and copies ran while one was open for 1% -> 0% of each run, Pallas kernels for 0% -> 0%
where the time goes in v1:
time: 30.6 us; the launch traced here: 30.2 us
  Pallas kernels  23.9 us (78%)
  local copies, waits for them, and re-layouts  6.32 us (21%)
    pallas_call x1, Pallas kernels, on_device(): pl.pallas_call(functools.partial(kernel, n_grp, n_loc), out_shape=jax.Sha...  23.9 us
    unnamed x17, local copies, waits for them, and re-layouts  6.32 us

profile of v1, /device:TPU:0, one launch (start us, length us, event | category | flops | bytes accessed | tf_op | source)
XLA Modules:
  0.0 30.2 jit_solution(2184777672496516677)
XLA Ops:
  0.0 0.0 copy-start.4
  0.0 0.0 copy-start.6
  0.0 0.0 copy-start.7
  0.0 0.7 %copy-done.4 = s32[1024]{0:T(1024)S(1)} copy-done((s32[1024]{0:T(1024)S(1)}, s32[1024]{0:T(1024)}, u32[]{:S(2)}) %copy-start.4) | copy-done | bytes 4120
  0.7 0.0 copy-done.6
  0.7 0.0 copy-done.7
  0.7 0.0 copy-start
  0.7 1.2 %copy-done = f32[1024,256]{1,0:T(8,128)S(1)} copy-done((f32[1024,256]{1,0:T(8,128)S(1)}, f32[1024,256]{1,0:T(8,128)}, u32[]{:S(2)}) %copy-start) | copy-done | bytes 1048600
  1.9 0.0 copy-start.1
  1.9 0.9 %copy-done.1 = bf16[128,1024]{1,0:T(8,128)(2,1)S(1)} copy-done((bf16[128,1024]{1,0:T(8,128)(2,1)S(1)}, bf16[128,1024]{1,0:T(8,128)(2,1)}, u32[]{:S(2)}) %copy-start.1) | copy-done | bytes 262168
  2.9 0.0 copy-start.2
  2.9 0.9 %copy-done.2 = f32[256,256]{1,0:T(8,128)S(1)} copy-done((f32[256,256]{1,0:T(8,128)S(1)}, f32[256,256]{1,0:T(8,128)}, u32[]{:S(2)}) %copy-start.2) | copy-done | bytes 262168
  3.8 0.0 copy-start.3
  3.8 0.8 %copy-done.3 = s32[1024,16]{0,1:T(8,128)S(1)} copy-done((s32[1024,16]{0,1:T(8,128)S(1)}, s32[1024,16]{0,1:T(8,128)}, u32[]{:S(2)}) %copy-start.3) | copy-done | bytes 65560
  4.7 0.0 copy-start.5
  4.7 0.7 %copy-done.5 = s32[8,128]{1,0:T(8,128)S(1)} copy-done((s32[8,128]{1,0:T(8,128)S(1)}, s32[8,128]{1,0:T(8,128)}, u32[]{:S(2)}) %copy-start.5) | copy-done | bytes 4120
  5.4 23.9 %shard_map.82 = f32[1024,256]{1,0:T(8,128)S(1)} custom-call(f32[1024,256]{1,0:T(8,128)S(1)} %copy-done, bf16[128,1024]{1,0:T(8,128)(2,1)S(1)} %copy-done.1, s32[4]{0:T(128)S(1)} %copy-done.7, s32[16,1024]{1,0:T(8,128)S(1)} %bitcast.3, s32[1,1024]{1,0:T(1,128)S(1)} %bitcast.4, s32[8,128]{1,0:T(8,128)S(1)} %copy-done.5, f32[256,256]{1,0:T(8,128)S(1)} %copy-done.2, ...), custom_call_target="tpu_custom_call" | custom-call | tf_op jit(solution)/shard_map/pallas_call | solution.py:267
  29.3 1.0 %copy.10 = f32[1024,256]{1,0:T(8,128)} copy(f32[1024,256]{1,0:T(8,128)S(1)} %shard_map.82) | data formatting | bytes 2097152
Async XLA Ops:
  0.0 0.7 %copy-start.4 = (s32[1024]{0:T(1024)S(1)}, s32[1024]{0:T(1024)}, u32[]{:S(2)}) copy-start(s32[1024]{0:T(1024)} %param.12) | copy-start | bytes 12292
  0.0 0.7 %copy-start.6 = (f32[256]{0:T(256)S(1)}, f32[256]{0:T(256)}, u32[]{:S(2)}) copy-start(f32[256]{0:T(256)} %param.15) | copy-start | bytes 3076
  0.0 0.7 %copy-start.7 = (s32[4]{0:T(128)S(1)}, s32[4]{0:T(128)}, u32[]{:S(2)}) copy-start(s32[4]{0:T(128)} %slot_ref.1) | copy-start | bytes 52
  0.7 1.2 %copy-start = (f32[1024,256]{1,0:T(8,128)S(1)}, f32[1024,256]{1,0:T(8,128)}, u32[]{:S(2)}) copy-start(f32[1024,256]{1,0:T(8,128)} %feat_ref.1) | copy-start | bytes 3145732
  1.9 0.9 %copy-start.1 = (bf16[128,1024]{1,0:T(8,128)(2,1)S(1)}, bf16[128,1024]{1,0:T(8,128)(2,1)}, u32[]{:S(2)}) copy-start(bf16[128,1024]{1,0:T(8,128)(2,1)} %hub_ref.1) | copy-start | bytes 786436
  2.9 0.9 %copy-start.2 = (f32[256,256]{1,0:T(8,128)S(1)}, f32[256,256]{1,0:T(8,128)}, u32[]{:S(2)}) copy-start(f32[256,256]{1,0:T(8,128)} %w_ref.1) | copy-start | bytes 786436
  3.8 0.8 %copy-start.3 = (s32[1024,16]{0,1:T(8,128)S(1)}, s32[1024,16]{0,1:T(8,128)}, u32[]{:S(2)}) copy-start(s32[1024,16]{0,1:T(8,128)} %param.11) | copy-start | bytes 196612
  4.7 0.7 %copy-start.5 = (s32[8,128]{1,0:T(8,128)S(1)}, s32[8,128]{1,0:T(8,128)}, u32[]{:S(2)}) copy-start(s32[8,128]{1,0:T(8,128)} %halo_ref.1) | copy-start | bytes 12292

commit v2 on v1

--- a/solution.py
+++ b/solution.py
@@ -57,8 +57,9 @@
 
 def kernel(
     n_grp, n_loc,
-    feat_ref, hub_ref, slot_ref, nbr_ref, cnt_ref, halo_ref, w_ref, bias_ref,
+    feat_hbm, hub_hbm, slot_hbm, nbr_hbm, cnt_hbm, halo_hbm, w_hbm, bias_hbm,
     out_ref,
+    feat_ref, hub_ref, slot_ref, nbr_ref, cnt_ref, halo_ref, w_ref, bias_ref, loaded,
     fh, fl, ph, pl_, base, acc, adj, codes, lows, outgoing, recv, part, part_in, spread, spread_in,
     inv, wh, wl,
     halo_s, halo_r, grp_s, grp_r, loc_s, loc_r,
@@ -84,10 +85,20 @@
             barrier, inc=1, device_id={"grp": (grp + off) % n_grp}, device_id_type=pl.DeviceIdType.MESH
         )
 
+    halo_load, feat_load, hub_load, nbr_load, cnt_load, w_load, bias_load, slot_load = [
+        pltpu.make_async_copy(source, target, loaded.at[number])
+        for number, (source, target) in enumerate((
+            (halo_hbm, halo_ref), (feat_hbm, feat_ref), (hub_hbm, hub_ref), (nbr_hbm, nbr_ref),
+            (cnt_hbm, cnt_ref), (w_hbm, w_ref), (bias_hbm, bias_ref), (slot_hbm, slot_ref),
+        ))
+    ]
+    for load in (halo_load, feat_load, hub_load, nbr_load, cnt_load, w_load, bias_load, slot_load):
+        load.start()
+    halo_load.wait()
+    feat_load.wait()
     high, low = split(feat_ref[...])
     fh[...] = high
     fl[...] = low
-    part[...] = dot(hub_ref[...], fh[...])
 
     def gather(peer):
         line = halo_ref[pl.ds(peer, 1), :]
@@ -134,13 +145,18 @@
     outgoing[order[0]] = gather(flip(me, order[0], n_loc))
     pl.semaphore_wait(barrier, n_loc - 1 + n_grp - 1)
     halo_copy(order[0]).start()
-    for off in range(1, n_grp):
-        grp_copy(off).start()
-    for off in order[1:]:
+    for number, off in enumerate(order[1:]):
         outgoing[off] = gather(flip(me, off, n_loc))
         halo_copy(off).start()
+        if number == 0:
+            hub_load.wait()
+            part[...] = dot(hub_ref[...], fh[...])
+            for grp_off in range(1, n_grp):
+                grp_copy(grp_off).start()
     recv[pl.ds(pl.multiple_of(me * listed, listed), listed), :] = gather(me)
 
+    nbr_load.wait()
+    cnt_load.wait()
     slot = nbr_ref[...]
     used = iota((slots, rows), 0) < jnp.broadcast_to(cnt_ref[...], (slots, rows))
     level = jnp.where(used, lax.shift_right_logical(slot, 7), -16).astype(F32)
@@ -157,6 +173,8 @@
     lows[...] = flatten(place).astype(jnp.int32)
     inv[...] = 1.0 / jnp.transpose(jnp.broadcast_to(cnt_ref[...].astype(F32), (8, rows)))
 
+    w_load.wait()
+    bias_load.wait()
     w_high, w_low = split(w_ref[...])
     wh[...] = w_high
     wl[...] = w_low
@@ -171,6 +189,7 @@
     pl_[...] = p_low
 
     group = 4
+    own = rows // 256
 
     def build(step, carry):
         for inner in range(group):
@@ -182,14 +201,16 @@
             counted = dot_nt(left, right).astype(BF)
             at = pl.ds(pl.multiple_of(block * per_block, per_block), per_block)
             for tile in range(levels):
-                adj[tile // 2, at, (tile % 2) * LANES:(tile % 2 + 1) * LANES] = counted[
-                    tile * per_block:(tile + 1) * per_block
-                ]
+                piece = counted[tile * per_block:(tile + 1) * per_block]
+                if tile < 2 * own:
+                    adj[tile // 2, at, (tile % 2) * LANES:(tile % 2 + 1) * LANES] = piece
+                else:
+                    adj[tile - own, at, 0:LANES] = piece
+                    adj[tile - own, at, LANES:2 * LANES] = piece
         return carry
 
     lax.fori_loop(0, blocks // group, build, 0)
 
-    own = rows // 256
     total = dot(adj[0], ph[0:256]) + dot(adj[0], pl_[0:256])
     for chunk in range(1, own):
         at = slice(chunk * 256, (chunk + 1) * 256)
@@ -207,23 +228,17 @@
     for off in range(1, n_loc):
         loc_copy(off).start()
 
-    def take(chip_off):
-        chip = flip(me // 2, chip_off, n_loc // 2)
-        got = recv[pl.ds(pl.multiple_of(chip * 2 * listed, 2 * listed), 2 * listed), :]
+    def take(off):
+        peer = flip(me, off, n_loc)
+        got = recv[pl.ds(pl.multiple_of(peer * listed, listed), listed), :]
         r_high, r_low = split(times_weight(*split(got)))
-        counts_of = adj[own + chip]
-        return dot(counts_of, r_high) + dot(counts_of, r_low)
-
-    chips = [0]
-    for off in order:
-        if off // 2 not in chips:
-            chips.append(off // 2)
-    halo_copy(1).wait_recv()
-    for chip_off in chips[:-1]:
-        if chip_off > 0:
-            halo_copy(2 * chip_off).wait_recv()
-            halo_copy(2 * chip_off + 1).wait_recv()
-        acc[...] += take(chip_off)
+        return dot(adj[own + peer], jnp.concatenate([r_high, r_low], axis=0))
+
+    acc[...] += take(0)
+    arrivals = [1] + order[:-1]
+    for off in arrivals[:-1]:
+        halo_copy(off).wait_recv()
+        acc[...] += take(off)
 
     hubs = spread[me]
     for off in range(1, n_loc):
@@ -231,6 +246,7 @@
         hubs = hubs + spread_in[off]
     hubs = jnp.concatenate([hubs, jnp.zeros((LANES - hubs.shape[0], width), F32)], axis=0)
     h_high, h_low = split(times_weight(*split(hubs)))
+    slot_load.wait()
     lane = iota((1, LANES), 1)
     target_row = jnp.full((1, LANES), -1, jnp.int32)
     for hub in range(hub_dev):
@@ -238,9 +254,8 @@
     here = onehot(iota((rows, LANES), 0) == target_row)
     base[...] += dot(here, h_high) + dot(here, h_low)
 
-    last = chips[-1]
-    halo_copy(2 * last).wait_recv()
-    halo_copy(2 * last + 1).wait_recv()
+    last = arrivals[-1]
+    halo_copy(last).wait_recv()
     out_ref[...] = jnp.maximum((acc[...] + take(last)) * inv[:, 0:1] + base[...], 0.0)
 
     for off in range(1, n_loc):
@@ -258,25 +273,33 @@
         slots = neighbours.shape[1]
         listed = halo_send.shape[1]
         hubs = hub_block.shape[0]
-        pool = rows + n_loc * listed
         blocks = rows // (256 // slots)
         padded = -(-hub_slot.shape[0] // 8) * 8
         vmem = pl.BlockSpec(memory_space=pltpu.VMEM)
-        smem = pl.BlockSpec(memory_space=pltpu.SMEM)
+        far = pl.BlockSpec(memory_space=pltpu.HBM)
         sem = pltpu.SemaphoreType.DMA
         return pl.pallas_call(
             functools.partial(kernel, n_grp, n_loc),
             out_shape=jax.ShapeDtypeStruct((rows, width), F32),
-            in_specs=[vmem, vmem, smem, vmem, vmem, vmem, vmem, vmem],
+            in_specs=[far] * 8,
             out_specs=vmem,
             scratch_shapes=[
+                pltpu.VMEM(features.shape, F32),
+                pltpu.VMEM(hub_block.shape, BF),
+                pltpu.SMEM(hub_slot.shape, jnp.int32),
+                pltpu.VMEM((slots, rows), jnp.int32),
+                pltpu.VMEM((1, rows), jnp.int32),
+                pltpu.VMEM(halo_send.shape, jnp.int32),
+                pltpu.VMEM(weight.shape, F32),
+                pltpu.VMEM((1, width), F32),
+                sem((8,)),
                 pltpu.VMEM((rows, width), BF),
                 pltpu.VMEM((rows, width), BF),
                 pltpu.VMEM((rows, width), BF),
                 pltpu.VMEM((rows, width), BF),
                 pltpu.VMEM((rows, width), F32),
                 pltpu.VMEM((rows, width), F32),
-                pltpu.VMEM((pool // 256, rows, 256), BF),
+                pltpu.VMEM((rows // 256 + n_loc, rows, 256), BF),
                 pltpu.VMEM((blocks, 256), jnp.int32),
                 pltpu.VMEM((blocks, 256), jnp.int32),
                 pltpu.VMEM((n_loc, listed, width), F32),
@@ -294,8 +317,13 @@
                 collective_id=0, has_side_effects=True, vmem_limit_bytes=48 * 1024 * 1024
             ),
         )(
-            features, hub_block, hub_slot, neighbours.T, counts.reshape(1, -1), halo_send, weight,
-            bias.reshape(1, -1),
+            *[
+                pltpu.with_memory_space_constraint(array, pltpu.HBM)
+                for array in (
+                    features, hub_block, hub_slot, neighbours.T, counts.reshape(1, -1), halo_send, weight,
+                    bias.reshape(1, -1),
+                )
+            ]
         )
 
     both = ("grp", "loc")

time: 30.6 us -> 24.8 us (0.81)
  local copies, waits for them, and re-layouts: 6.32 us -> 0.97 us
    unnamed x17 -> x1, local copies, waits for them, and re-layouts: 6.32 us -> 0.97 us
where the time goes in v2:
time: 24.8 us; the launch traced here: 24.6 us
  Pallas kernels  23.7 us (96%)
  local copies, waits for them, and re-layouts  0.97 us (4%)
    pallas_call x1, Pallas kernels, on_device(): pl.pallas_call(functools.partial(kernel, n_grp, n_loc), out_shape=jax.Sha...  23.7 us
    unnamed x1, local copies, waits for them, and re-layouts  0.97 us

profile of v2, /device:TPU:0, one launch (start us, length us, event | category | flops | bytes accessed | tf_op | source)
XLA Modules:
  0.0 24.6 jit_solution(2731270021977181733)
XLA Ops:
  0.0 23.7 %shard_map.82 = f32[1024,256]{1,0:T(8,128)S(1)} custom-call(f32[1024,256]{1,0:T(8,128)} %feat_hbm.1, bf16[128,1024]{1,0:T(8,128)(2,1)} %hub_hbm.1, s32[4]{0:T(128)} %slot_hbm.1, s32[16,1024]{1,0:T(8,128)} %bitcast.3, s32[1,1024]{1,0:T(1,128)} %bitcast.4, s32[8,128]{1,0:T(8,128)} %halo_hbm.1, f32[256,256]{1,0:T(8,128)} %w_hbm.1, f32[1,256]{1,0:T(1,128)} %bitcast.5), custom_call_target="tpu_custom_call" | custom-call | tf_op jit(solution)/shard_map/pallas_call | solution.py:281
  23.7 1.0 %copy.10 = f32[1024,256]{1,0:T(8,128)} copy(f32[1024,256]{1,0:T(8,128)S(1)} %shard_map.82) | data formatting | bytes 2097152
